TPU v7x, 32 devices: a whole 2x2x4 slice. The times are simulated.
32 devices in a mesh: gx: 2 (over x), gy: 4 (over z), gz: 4 (over y, core).
Axes of the slice: x: 2, y: 2, z: 4, core: 2. Of those that a mesh axis runs over, the one named last changes fastest.
Arguments:
- pair_list: int32 [1024, 2], P(('gx', 'gy', 'gz')), may hold values from 0 to 63, all different within a row; in each aligned block of 32 rows (0 to 31, 32 to 63, ...) at most 2 rows name the same one
- rank_bucket: int32 [1024], P(('gx', 'gy', 'gz')), may hold values from 0 to 2
- amplitudes: bfloat16 [1024, 36864], P(('gx', 'gy', 'gz')), may hold values from -0.4375 to 0.4375
- intersects: bfloat16 [1024, 36864], P(('gx', 'gy', 'gz')), may hold values from -0.4375 to 0.4375
- integrals: bfloat16 [1024, 36864], P(('gx', 'gy', 'gz')), may hold values from -6 to 6
- exchange_blocks: bfloat16 [64, 36864], P(('gx', 'gy')), may hold values from -0.4375 to 0.4375
Outputs:
- residuals: bfloat16 [1024, 36864], P(('gx', 'gy', 'gz'))
Inputs may be any that keep to these rules, and one draw needn't show every extreme that they name: `pair_list`: each row names two different occupied orbitals; within the rows of one device no orbital is named more than 2 times, a bound that some block reaches on some devices. `rank_bucket`: bucket b keeps the leading (b + 1) * 64 PNOs.
All inputs are finite; a program needn't handle non-finite values.
Results may differ from a plain program's by a relative error of at most 0.013.
Values may be sent and summed in bfloat16 or wider, within the bound.
A program may use at most 128 MiB of HBM per device.

v0:
```python
import jax
import jax.numpy as jnp
from jax import lax
from jax.sharding import PartitionSpec as P

RSTEP = 64
R = 192


def body(pair_list, rank_bucket, amplitudes, intersects, integrals, exchange_blocks):
    pair_rows = amplitudes.shape[0]
    rank_width = R
    owned_rows = exchange_blocks.shape[0]
    amplitudes = amplitudes.reshape(pair_rows, rank_width, rank_width)
    intersects = intersects.reshape(pair_rows, rank_width, rank_width)
    integrals = integrals.reshape(pair_rows, rank_width, rank_width)
    exchange_blocks = exchange_blocks.reshape(owned_rows, rank_width, rank_width)
    groups_x, groups_y = (lax.axis_size("gx"), lax.axis_size("gy"))
    group_total = groups_x * groups_y
    occupied = owned_rows * group_total
    row_index = lax.broadcasted_iota(jnp.int32, (rank_width, rank_width), 0)
    col_index = lax.broadcasted_iota(jnp.int32, (rank_width, rank_width), 1)
    pair_rank = (rank_bucket + 1) * RSTEP
    inside = (row_index[None] < pair_rank[:, None, None]) & (
        col_index[None] < pair_rank[:, None, None]
    )
    masked = jnp.where(inside, amplitudes, jnp.zeros_like(amplitudes))
    half_projected = jnp.einsum(
        "pab,pbc->pac", intersects, masked, preferred_element_type=jnp.float32
    ).astype(jnp.bfloat16)
    projected = jnp.einsum(
        "pab,pcb->pac", half_projected, intersects, preferred_element_type=jnp.float32
    ).astype(jnp.bfloat16)
    local_term = jnp.einsum("pab,pbc->pac", masked, integrals, preferred_element_type=jnp.float32)
    flat_projected = projected.reshape(pair_rows, rank_width * rank_width)
    end_counts = jnp.sum(
        (pair_list[None] == lax.broadcasted_iota(jnp.int32, (occupied, 1, 1), 0)).astype(jnp.int32),
        axis=2,
    ).astype(jnp.bfloat16)
    partial_sum = lax.psum_scatter(
        jnp.dot(end_counts, flat_projected, preferred_element_type=jnp.float32),
        ("gx", "gy"),
        scatter_dimension=0,
        tiled=True,
    ).reshape(owned_rows, rank_width, rank_width)
    domain = lax.psum(partial_sum, "gz")
    coupled = jnp.einsum(
        "oab,obc->oac",
        domain.astype(jnp.bfloat16),
        exchange_blocks,
        preferred_element_type=jnp.float32,
    ).astype(jnp.bfloat16)
    every_coupled, every_block = (
        lax.all_gather(coupled, ("gx", "gy"), axis=0, tiled=True),
        lax.all_gather(exchange_blocks, ("gx", "gy"), axis=0, tiled=True),
    )
    picked_blocks = every_block[pair_list]
    picked_coupled = every_coupled[pair_list]
    own_term = jnp.einsum(
        "pab,pebc->peac", projected, picked_blocks, preferred_element_type=jnp.float32
    ).astype(jnp.bfloat16)
    answers = (picked_coupled.astype(jnp.float32) - own_term.astype(jnp.float32)).astype(
        jnp.bfloat16
    )
    combined = (answers[:, 0].astype(jnp.float32) + answers[:, 1].astype(jnp.float32)).astype(
        jnp.bfloat16
    )
    half_back = jnp.einsum(
        "pba,pbc->pac", intersects, combined, preferred_element_type=jnp.float32
    ).astype(jnp.bfloat16)
    back_projected = jnp.einsum(
        "pab,pbc->pac", half_back, intersects, preferred_element_type=jnp.float32
    )
    residual_sum = integrals.astype(jnp.float32) + local_term + back_projected
    result = jnp.where(inside, residual_sum, jnp.zeros_like(residual_sum)).astype(jnp.bfloat16)
    return result.reshape(pair_rows, rank_width * rank_width)


def solution(mesh):
    placed = (
        P(("gx", "gy", "gz"), None),
        P(("gx", "gy", "gz")),
        P(("gx", "gy", "gz"), None),
        P(("gx", "gy", "gz"), None),
        P(("gx", "gy", "gz"), None),
        P(("gx", "gy"), None),
    )
    return jax.shard_map(
        body, mesh=mesh, in_specs=placed, out_specs=P(("gx", "gy", "gz"), None), check_vma=False
    )
```

profile of v0, /device:TPU:0, one launch (start us, length us, event | category | flops | bytes accessed | tf_op | source)
XLA Modules:
  0.0 454.9 jit_solution(4188154951140406437)
XLA Ops:
  6.5 6.1 %reshape.28 = bf16[32,192,192]{2,1,0:T(8,128)(2,1)} reshape(bf16[32,36864]{1,0:T(8,128)(2,1)} %param.8) | data formatting | bytes 4718592 | tf_op jit(solution)/shard_map/reshape | solution.py:14
  12.7 5.0 %reshape.29 = bf16[32,192,192]{2,1,0:T(8,128)(2,1)S(1)} reshape(bf16[32,36864]{1,0:T(8,128)(2,1)} %param.9) | data formatting | bytes 4718592 | tf_op jit(solution)/shard_map/reshape | solution.py:15
  17.7 6.9 %fusion.19 = bf16[32,192,192]{2,1,0:T(8,128)(2,1)} fusion(bf16[32,192,192]{2,1,0:T(8,128)(2,1)S(1)} %reshape.29, bf16[32,192,192]{2,1,0:T(8,128)(2,1)} %reshape.28, s32[32]{0:T(128)S(1)} %add_multiply_fusion), kind=kOutput, calls=%fused_computation.20 | convolution fusion | flops 913047552 | bytes 7078016 | tf_op jit(solution)/shard_map/pab,pcb->pac/dot_general | solution.py:31
  24.5 6.2 %reshape.30 = bf16[32,36864]{1,0:T(8,128)(2,1)} reshape(bf16[32,192,192]{2,1,0:T(8,128)(2,1)} %fusion.19) | data formatting | bytes 4718592 | tf_op jit(solution)/shard_map/reshape | solution.py:35
  30.7 0.1 convert_reduce_fusion
  30.8 6.7 %fusion.26 = f32[64,36864]{1,0:T(8,128)} fusion(bf16[32,36864]{1,0:T(8,128)(2,1)} %reshape.30, s32[64,32]{0,1:T(8,128)S(1)} %convert_reduce_fusion), kind=kOutput, calls=%fused_computation.25 | convolution fusion | flops 150996992 | bytes 11804672 | tf_op jit(solution)/shard_map/dot_general | solution.py:41
  37.5 0.0 all-gather.5.cloned.1.call-start
  37.5 2.9 reshape.32
  40.5 162.0 %reduce-scatter.2.cloned.1.call-done = f32[8,36864]{1,0:T(8,128)} async-done(((f32[64,36864]{1,0:T(8,128)}), f32[8,36864]{1,0:T(8,128)}) %reduce-scatter.2.cloned.1.call-update) | async-done | bytes 1179664 | tf_op jit(solution)/shard_map/reduce_scatter | solution.py:40
  202.5 3.1 reshape.31
  205.6 34.0 %all-reduce.1 = bf16[8,192,192]{2,1,0:T(8,128)(2,1)} all-reduce(f32[8,192,192]{2,1,0:T(8,128)} %reshape.31), channel_id=1, replica_groups=mesh['gx'=2,'gy'=4,'gz'=4] {'gz'}, use_global_device_ids=true, to_apply=%region_2.3 | all-reduce | flops 294912 | bytes 1769472 | tf_op jit(solution)/shard_map/psum | solution.py:46
  239.6 2.6 convolution_convert_fusion
  242.2 0.1 copy.24
  242.3 0.1 reshape.36
  242.4 6.3 %reshape.27 = bf16[32,192,192]{2,1,0:T(8,128)(2,1)} reshape(bf16[32,36864]{1,0:T(8,128)(2,1)} %param.10) | data formatting | bytes 4718592 | tf_op jit(solution)/shard_map/reshape | solution.py:16
  248.7 53.7 %all-gather.5.cloned.1.call-done = bf16[64,192,192]{2,1,0:T(8,128)(2,1)} async-done(((bf16[8,192,192]{2,1,0:T(8,128)(2,1)}), bf16[64,192,192]{2,1,0:T(8,128)(2,1)}) %all-gather.5.cloned.1.call-update) | async-done | bytes 4718608 | tf_op jit(solution)/shard_map/all_gather | solution.py:55
  302.4 6.3 %gather_fusion.1 = bf16[64,192,192]{2,1,0:T(8,128)(2,1)} fusion(bf16[64,192,192]{2,1,0:T(8,128)(2,1)} %all-gather.5.cloned.1.call-done, s32[1024]{0:T(1024)S(1)} %pad_clamp_fusion), kind=kCustom, calls=%fused_computation.1 | custom fusion | bytes 9437440 | tf_op jit(solution)/shard_map/gather | solution.py:57
  308.7 92.7 %all-gather.3.cloned.1.call-done = bf16[64,192,192]{2,1,0:T(8,128)(2,1)} async-done(((bf16[8,192,192]{2,1,0:T(8,128)(2,1)}), bf16[64,192,192]{2,1,0:T(8,128)(2,1)}) %all-gather.3.cloned.1.call-update) | async-done | bytes 4718608 | tf_op jit(solution)/shard_map/all_gather | solution.py:54
  401.4 6.4 %gather_fusion = bf16[64,192,192]{2,1,0:T(8,128)(2,1)} fusion(bf16[64,192,192]{2,1,0:T(8,128)(2,1)} %all-gather.3.cloned.1.call-done, s32[1024]{0:T(1024)S(1)} %pad_clamp_fusion), kind=kCustom, calls=%fused_computation | custom fusion | bytes 9437440 | tf_op jit(solution)/shard_map/gather | solution.py:58
  407.9 9.7 %copy.25 = f32[64,192,192]{1,2,0:T(8,128)} copy(bf16[64,192,192]{2,1,0:T(8,128)(2,1)} %gather_fusion) | data formatting | bytes 14155776 | tf_op jit(solution)/shard_map/convert_element_type | solution.py:62
  417.5 11.3 %fusion = bf16[32,2,192,192]{2,3,1,0:T(8,128)(2,1)} fusion(f32[32,2,192,192]{2,3,1,0:T(8,128)} %bitcast.27, bf16[32,2,192,192]{3,2,1,0:T(8,128)(2,1)} %bitcast.28, bf16[32,192,192]{2,1,0:T(8,128)(2,1)} %fusion.19), kind=kOutput, calls=%fused_computation.3 | convolution fusion | flops 915406848 | bytes 21233664 | tf_op jit(solution)/shard_map/pab,pebc->peac/dot_general | solution.py:59
  428.8 7.5 %fusion.9 = f32[32,192,192]{2,1,0:T(8,128)} fusion(bf16[32,192,192]{2,1,0:T(8,128)(2,1)S(1)} %reshape.29, bf16[32,2,192,192]{2,3,1,0:T(8,128)(2,1)} %fusion), kind=kOutput, calls=%fused_computation.15 | convolution fusion | flops 911867904 | bytes 15728640 | tf_op jit(solution)/shard_map/pab,pbc->pac/dot_general | solution.py:71
  436.3 7.9 %select_convert_fusion = bf16[32,192,192]{2,1,0:T(8,128)(2,1)S(1)} fusion(f32[32,192,192]{2,1,0:T(8,128)} %fusion.9, bf16[32,192,192]{2,1,0:T(8,128)(2,1)} %reshape.27, s32[32]{0:T(128)S(1)} %add_multiply_fusion, bf16[32,192,192]{2,1,0:T(8,128)(2,1)} %reshape.28), kind=kOutput, calls=%fused_computation.4 | convolution fusion | flops 467140608 | bytes 11796608 | tf_op jit(solution)/shard_map/pab,pbc->pac/dot_general | solution.py:34
  444.1 4.2 reshape.33
  (12 shorter events, 0.1 us)
Async XLA Ops:
  6.5 195.9 %reduce-scatter.2.cloned.1.call-start = ((), (), s32[]{:S(2)}) async-start(), calls=%async_computation.1 | async-start | bytes 10616832 | tf_op jit(solution)/shard_map/reduce_scatter | solution.py:40
  12.7 5.0 %copy-start.1 = (s32[32]{0:T(128)S(1)}, s32[32]{0:T(128)}, u32[]{:S(2)}) copy-start(s32[32]{0:T(128)} %param.7) | copy-start | bytes 388
  24.5 6.2 %copy-start = (s32[32,2]{0,1:T(2,128)S(1)}, s32[32,2]{0,1:T(2,128)}, u32[]{:S(2)}) copy-start(s32[32,2]{0,1:T(2,128)} %param.6) | copy-start | bytes 772
  37.5 264.9 %all-gather.5.cloned.1.call-start = ((), (), s32[]{:S(2)}) async-start(), calls=%async_computation.3 | async-start | bytes 7077888 | tf_op jit(solution)/shard_map/all_gather | solution.py:55
  40.5 361.0 %all-gather.3.cloned.1.call-start = ((), (), s32[]{:S(2)}) async-start(), calls=%async_computation.2 | async-start | bytes 7077888 | tf_op jit(solution)/shard_map/all_gather | solution.py:54
Sparse Core Ops, SparseCore 0:
  37.6 164.8 reduce-scatter.1
  204.6 97.7 all-gather.4
  304.5 96.8 all-gather.2
where the time goes:
time: 456 us; the launch traced here: 455 us
  waiting for transfers between devices  308 us (68%)
  local copies, waits for them, and re-layouts  56.5 us (12%)
  matrix products  42.8 us (9%)
  blocking collectives  34 us (7%)
  between operations  13.2 us (3%)
    reduce_scatter x1, waiting for transfers between devices, body(): lax.psum_scatter(jnp.dot(end_counts, flat_projected, preferred_element_ty...  162 us
    all_gather x1, waiting for transfers between devices, body(): lax.all_gather(coupled, ('gx', 'gy'), axis=0, tiled=True)  92.7 us
    all_gather x1, waiting for transfers between devices, body(): lax.all_gather(exchange_blocks, ('gx', 'gy'), axis=0, tiled=True)  53.7 us
    psum x1, blocking collectives, body(): domain = lax.psum(partial_sum, 'gz')  34 us
    dot_general x1, matrix products, body(): jnp.einsum('pab,pebc->peac', projected, picked_blocks, preferred_element_...  11.3 us
    convert_element_type x1, local copies, waits for them, and re-layouts, body(): picked_coupled.astype(jnp.float32) - own_term.astype(jnp.float32)  9.66 us
  transfers between devices with their start and end apart: 3, of which 3 were waited for; matrix products, arithmetic and copies ran while one was open for 5% of the time, Pallas kernels for 0%

commit v1 on v0

--- a/solution.py
+++ b/solution.py
@@ -43,7 +43,10 @@
         scatter_dimension=0,
         tiled=True,
     ).reshape(owned_rows, rank_width, rank_width)
-    domain = lax.psum(partial_sum, "gz")
+    size, domain = (lax.axis_size("gz"), partial_sum)
+    for stride in [1 << k for k in range(size.bit_length() - 1)]:
+        swap = [(i, i ^ stride) for i in range(size)]
+        domain = domain + lax.ppermute(domain, "gz", swap)
     coupled = jnp.einsum(
         "oab,obc->oac",
         domain.astype(jnp.bfloat16),

time: 456 us -> 456 us (level)
  blocking collectives: 34 us -> 0 us
  waiting for transfers between devices: 308 us -> 341 us
    ppermute x0 -> x2, waiting for transfers between devices: none -> 38.6 us  [body(): domain = domain + lax.ppermute(domain, 'gz', swap)]
    psum x1 -> x0, blocking collectives: 34 us -> none  [body(): domain = lax.psum(partial_sum, 'gz')]
    all_gather x1, waiting for transfers between devices: 53.7 us -> 47.4 us  [body(): lax.all_gather(exchange_blocks, ('gx', 'gy'), axis=0, tiled=True)]
  transfers between devices with their start and end apart: 3 -> 5, of which waited for: 3 -> 5; matrix products, arithmetic and copies ran while one was open for 5% -> 5% of each run, Pallas kernels for 0% -> 0%
where the time goes in v1:
time: 456 us; the launch traced here: 455 us
  waiting for transfers between devices  341 us (75%)
  local copies, waits for them, and re-layouts  56.2 us (12%)
  matrix products  41.6 us (9%)
  between operations  13.2 us (3%)
    reduce_scatter x1, waiting for transfers between devices, body(): lax.psum_scatter(jnp.dot(end_counts, flat_projected, preferred_element_ty...  162 us
    all_gather x1, waiting for transfers between devices, body(): lax.all_gather(coupled, ('gx', 'gy'), axis=0, tiled=True)  92.7 us
    all_gather x1, waiting for transfers between devices, body(): lax.all_gather(exchange_blocks, ('gx', 'gy'), axis=0, tiled=True)  47.4 us
    ppermute x2, waiting for transfers between devices, body(): domain = domain + lax.ppermute(domain, 'gz', swap)  38.6 us
    dot_general x1, matrix products, body(): jnp.einsum('pab,pebc->peac', projected, picked_blocks, preferred_element_...  11.3 us
    convert_element_type x1, local copies, waits for them, and re-layouts, body(): picked_coupled.astype(jnp.float32) - own_term.astype(jnp.float32)  9.69 us
  transfers between devices with their start and end apart: 5, of which 5 were waited for; matrix products, arithmetic and copies ran while one was open for 5% of the time, Pallas kernels for 0%

profile of v1, /device:TPU:0, one launch (start us, length us, event | category | flops | bytes accessed | tf_op | source)
XLA Modules:
  0.0 455.0 jit_solution(6547689980813636764)
XLA Ops:
  6.5 6.1 %reshape.28 = bf16[32,192,192]{2,1,0:T(8,128)(2,1)} reshape(bf16[32,36864]{1,0:T(8,128)(2,1)} %param.8) | data formatting | bytes 4718592 | tf_op jit(solution)/shard_map/reshape | solution.py:14
  12.7 5.0 %reshape.29 = bf16[32,192,192]{2,1,0:T(8,128)(2,1)S(1)} reshape(bf16[32,36864]{1,0:T(8,128)(2,1)} %param.9) | data formatting | bytes 4718592 | tf_op jit(solution)/shard_map/reshape | solution.py:15
  17.7 6.9 %fusion.19 = bf16[32,192,192]{2,1,0:T(8,128)(2,1)} fusion(bf16[32,192,192]{2,1,0:T(8,128)(2,1)S(1)} %reshape.29, bf16[32,192,192]{2,1,0:T(8,128)(2,1)} %reshape.28, s32[32]{0:T(128)S(1)} %add_multiply_fusion), kind=kOutput, calls=%fused_computation.20 | convolution fusion | flops 913047552 | bytes 7078016 | tf_op jit(solution)/shard_map/pab,pcb->pac/dot_general | solution.py:31
  24.6 6.2 %reshape.30 = bf16[32,36864]{1,0:T(8,128)(2,1)} reshape(bf16[32,192,192]{2,1,0:T(8,128)(2,1)} %fusion.19) | data formatting | bytes 4718592 | tf_op jit(solution)/shard_map/reshape | solution.py:35
  30.8 6.7 %fusion.25 = f32[64,36864]{1,0:T(8,128)} fusion(bf16[32,36864]{1,0:T(8,128)(2,1)} %reshape.30, s32[64,32]{0,1:T(8,128)S(1)} %convert_reduce_fusion), kind=kOutput, calls=%fused_computation.25 | convolution fusion | flops 150996992 | bytes 11804672 | tf_op jit(solution)/shard_map/dot_general | solution.py:41
  37.6 2.9 reshape.32
  40.5 0.2 all-gather.3.cloned.1.call-start
  40.8 161.8 %reduce-scatter.2.cloned.1.call-done = f32[8,36864]{1,0:T(8,128)} async-done(((f32[64,36864]{1,0:T(8,128)}), f32[8,36864]{1,0:T(8,128)}) %reduce-scatter.2.cloned.1.call-update) | async-done | bytes 1179664 | tf_op jit(solution)/shard_map/reduce_scatter | solution.py:40
  202.6 3.1 reshape.31
  205.7 3.6 collective-permute-done
  209.3 1.6 add.31
  210.9 1.5 collective-permute-start.1
  212.5 35.0 %collective-permute-done.1 = f32[8,192,192]{2,1,0:T(8,128)S(1)} collective-permute-done((f32[8,192,192]{2,1,0:T(8,128)S(1)}, f32[8,192,192]{2,1,0:T(8,128)S(1)}, u32[]{:S(2)}, u32[]{:S(2)}) %collective-permute-start.1) | collective-permute-done | bytes 1179680 | tf_op jit(solution)/shard_map/ppermute | solution.py:49
  247.4 1.3 convolution_convert_fusion
  248.9 6.1 %reshape.27 = bf16[32,192,192]{2,1,0:T(8,128)(2,1)} reshape(bf16[32,36864]{1,0:T(8,128)(2,1)} %param.10) | data formatting | bytes 4718592 | tf_op jit(solution)/shard_map/reshape | solution.py:16
  255.1 47.4 %all-gather.5.cloned.1.call-done = bf16[64,192,192]{2,1,0:T(8,128)(2,1)} async-done(((bf16[8,192,192]{2,1,0:T(8,128)(2,1)}), bf16[64,192,192]{2,1,0:T(8,128)(2,1)}) %all-gather.5.cloned.1.call-update) | async-done | bytes 4718608 | tf_op jit(solution)/shard_map/all_gather | solution.py:58
  302.5 6.3 %gather_fusion.1 = bf16[64,192,192]{2,1,0:T(8,128)(2,1)} fusion(bf16[64,192,192]{2,1,0:T(8,128)(2,1)} %all-gather.5.cloned.1.call-done, s32[1024]{0:T(1024)S(1)} %pad_clamp_fusion), kind=kCustom, calls=%fused_computation.1 | custom fusion | bytes 9437440 | tf_op jit(solution)/shard_map/gather | solution.py:60
  308.8 92.7 %all-gather.3.cloned.1.call-done = bf16[64,192,192]{2,1,0:T(8,128)(2,1)} async-done(((bf16[8,192,192]{2,1,0:T(8,128)(2,1)}), bf16[64,192,192]{2,1,0:T(8,128)(2,1)}) %all-gather.3.cloned.1.call-update) | async-done | bytes 4718608 | tf_op jit(solution)/shard_map/all_gather | solution.py:57
  401.5 6.3 %gather_fusion = bf16[64,192,192]{2,1,0:T(8,128)(2,1)} fusion(bf16[64,192,192]{2,1,0:T(8,128)(2,1)} %all-gather.3.cloned.1.call-done, s32[1024]{0:T(1024)S(1)} %pad_clamp_fusion), kind=kCustom, calls=%fused_computation | custom fusion | bytes 9437440 | tf_op jit(solution)/shard_map/gather | solution.py:61
  407.8 9.7 %copy.25 = f32[64,192,192]{1,2,0:T(8,128)} copy(bf16[64,192,192]{2,1,0:T(8,128)(2,1)} %gather_fusion) | data formatting | bytes 14155776 | tf_op jit(solution)/shard_map/convert_element_type | solution.py:65
  417.5 11.3 %fusion = bf16[32,2,192,192]{2,3,1,0:T(8,128)(2,1)} fusion(f32[32,2,192,192]{2,3,1,0:T(8,128)} %bitcast.26, bf16[32,2,192,192]{3,2,1,0:T(8,128)(2,1)} %bitcast.27, bf16[32,192,192]{2,1,0:T(8,128)(2,1)} %fusion.19), kind=kOutput, calls=%fused_computation.3 | convolution fusion | flops 915406848 | bytes 21233664 | tf_op jit(solution)/shard_map/pab,pebc->peac/dot_general | solution.py:62
  428.8 7.5 %fusion.9 = f32[32,192,192]{2,1,0:T(8,128)} fusion(bf16[32,192,192]{2,1,0:T(8,128)(2,1)S(1)} %reshape.29, bf16[32,2,192,192]{2,3,1,0:T(8,128)(2,1)} %fusion), kind=kOutput, calls=%fused_computation.15 | convolution fusion | flops 911867904 | bytes 15728640 | tf_op jit(solution)/shard_map/pab,pbc->pac/dot_general | solution.py:74
  436.4 7.9 %select_convert_fusion = bf16[32,192,192]{2,1,0:T(8,128)(2,1)S(1)} fusion(f32[32,192,192]{2,1,0:T(8,128)} %fusion.9, bf16[32,192,192]{2,1,0:T(8,128)(2,1)} %reshape.27, s32[32]{0:T(128)S(1)} %add_multiply_fusion, bf16[32,192,192]{2,1,0:T(8,128)(2,1)} %reshape.28), kind=kOutput, calls=%fused_computation.4 | convolution fusion | flops 467140608 | bytes 11796608 | tf_op jit(solution)/shard_map/pab,pbc->pac/dot_general | solution.py:34
  444.2 4.2 reshape.33
  (18 shorter events, 0.4 us)
Async XLA Ops:
  6.5 196.0 %reduce-scatter.2.cloned.1.call-start = ((), (), s32[]{:S(2)}) async-start(), calls=%async_computation.1 | async-start | bytes 10616832 | tf_op jit(solution)/shard_map/reduce_scatter | solution.py:40
  12.7 5.0 %copy-start.2 = (s32[32]{0:T(128)S(1)}, s32[32]{0:T(128)}, u32[]{:S(2)}) copy-start(s32[32]{0:T(128)} %param.7) | copy-start | bytes 388
  24.6 6.2 %copy-start.1 = (s32[32,2]{0,1:T(2,128)S(1)}, s32[32,2]{0,1:T(2,128)}, u32[]{:S(2)}) copy-start(s32[32,2]{0,1:T(2,128)} %param.6) | copy-start | bytes 772
  37.6 264.9 %all-gather.5.cloned.1.call-start = ((), (), s32[]{:S(2)}) async-start(), calls=%async_computation.3 | async-start | bytes 7077888 | tf_op jit(solution)/shard_map/all_gather | solution.py:58
  40.5 361.0 %all-gather.3.cloned.1.call-start = ((), (), s32[]{:S(2)}) async-start(), calls=%async_computation.2 | async-start | bytes 7077888 | tf_op jit(solution)/shard_map/all_gather | solution.py:57
  205.7 41.7 %copy-start = (bf16[8,192,192]{2,1,0:T(8,128)(2,1)S(1)}, bf16[8,192,192]{2,1,0:T(8,128)(2,1)}, u32[]{:S(2)}) copy-start(bf16[8,192,192]{2,1,0:T(8,128)(2,1)} %reshape.32) | copy-start | bytes 1769476
  205.7 3.6 collective-permute-start
  210.9 36.5 %collective-permute-start.1 = (f32[8,192,192]{2,1,0:T(8,128)S(1)}, f32[8,192,192]{2,1,0:T(8,128)S(1)}, u32[]{:S(2)}, u32[]{:S(2)}) collective-permute-start(f32[8,192,192]{2,1,0:T(8,128)S(1)} %add.31), channel_id=1, source_target_pairs={{0,2},{1,3},{2,0},{3,1},{4,6},{5,7},{6,4},{7,5},{8,10},{9,11},{10,... | collective-permute-start | bytes 3538952 | tf_op jit(solution)/shard_map/ppermute | solution.py:49
Sparse Core Ops, SparseCore 0:
  37.7 164.8 reduce-scatter.1
  204.6 97.7 all-gather.4
  304.6 96.8 all-gather.2
